TPU v7x, 128 devices: a whole 4x4x4 slice. The times are simulated.
128 devices in a mesh: row: 16 (over x, z), col: 8 (over y, core).
Axes of the slice: x: 4, y: 4, z: 4, core: 2. Of those that a mesh axis runs over, the one named last changes fastest.
Arguments:
- panel_block: float32 [20480, 512], P('row', 'col'), may hold values from -12 to 12
- trailing: float32 [20480, 20480], P('row', 'col'), may hold values from -6 to 6
Outputs:
- updated: float32 [20480, 20480], P('row', 'col')
All inputs are finite; a program needn't handle non-finite values.
Results may differ from a plain program's by a relative error of at most 0.0003.
Values sent between devices are 32-bit elements; how exact they have to be, the bound alone decides.
A program may use at most 128 MiB of HBM per device.

v0:
```python
import functools

import jax
import jax.numpy as jnp
from jax import lax
from jax.sharding import Mesh
from jax.sharding import PartitionSpec as P

N = 20480
ROW = ("row_0", "row_1")


def in_order(pieces, dim):
    pieces = jnp.moveaxis(pieces, 0, dim)
    lengths = pieces.shape
    return pieces.reshape(*lengths[:dim], lengths[dim] * lengths[dim + 1], *lengths[dim + 2 :])


def from_everyone(array, axis):
    copies = jnp.broadcast_to(array, (lax.axis_size(axis), *array.shape))
    return lax.all_to_all(copies, axis, split_axis=0, concat_axis=0, tiled=True)


def gather_directly(array, axis, dim):
    return in_order(from_everyone(array, axis), dim)


def one_axis_at_a_time(array, axes):
    return functools.reduce(lax.psum, axes, array)


def on_device(panel_block, trailing):
    local_rows = panel_block.shape[0]
    local_width = panel_block.shape[1]
    rows_count = lax.axis_size(ROW)
    cols_count = lax.axis_size("col")
    copies = rows_count // cols_count
    row_owner = lax.axis_index(ROW)
    col_owner = lax.axis_index("col")
    mc_rows = gather_directly(panel_block, "col", 1)
    squares = one_axis_at_a_time(jnp.sum(mc_rows * mc_rows), ROW)
    column_block = lax.all_gather(panel_block, ROW, axis=0, tiled=True)
    shaped = column_block.reshape(copies, cols_count, local_rows, local_width)
    moved = lax.all_to_all(shaped, "col", split_axis=1, concat_axis=3, tiled=True)
    stacked = moved.reshape(copies, local_rows, mc_rows.shape[1])
    mr_rows = jnp.transpose(stacked, (1, 0, 2)).reshape(copies * local_rows, stacked.shape[2])
    update = lax.dot_general(
        mc_rows,
        mr_rows,
        (((1,), (1,)), ((), ())),
        precision=lax.Precision.HIGHEST,
        preferred_element_type=jnp.float32,
    )
    row_index = jnp.arange(local_rows, dtype=jnp.int32) * rows_count + row_owner
    col_index = jnp.arange(mr_rows.shape[0], dtype=jnp.int32) * cols_count + col_owner
    lower_part = row_index[:, None] >= col_index[None, :]
    factor = 0.8 * jnp.sqrt(jnp.float32(N)) / jnp.sqrt(squares + 1e-06)
    return trailing - factor * jnp.where(lower_part, update, jnp.zeros_like(update))


def solution(mesh):
    split = Mesh(mesh.devices.reshape(4, 4, mesh.shape["col"]), ("row_0", "row_1", "col"))
    return jax.shard_map(
        on_device,
        mesh=split,
        in_specs=(P(ROW, "col"), P(ROW, "col")),
        out_specs=P(ROW, "col"),
        check_vma=False,
    )
```

profile of v0, /device:TPU:8, one launch (start us, length us, event | category | flops | bytes accessed | tf_op | source)
XLA Modules:
  0.0 217.6 jit_solution(12133369068866333797)
XLA Ops:
  6.5 0.0 all-gather.2.cloned.1.call-start
  6.5 0.7 all-gather.2.cloned.1.call-update
  7.3 2.7 %broadcast_in_dim.8 = f32[8,1280,64]{1,2,0:T(8,128)} broadcast(f32[1280,64]{0,1:T(8,128)} %param.2), dimensions={1,2} | broadcast | bytes 2949120 | tf_op jit(solution)/shard_map/broadcast_in_dim | solution.py:20
  9.9 4.9 %all-to-all-start = ((f32[8,1280,64]{1,2,0:T(8,128)}), f32[8,1280,64]{1,2,0:T(8,128)S(1)}, u32[]{:S(2)}, u32[]{:S(2)}) async-start(f32[8,1280,64]{1,2,0:T(8,128)} %broadcast_in_dim.8), calls=%async_computation | async-start | bytes 5242880 | tf_op jit(solution)/shard_map/all_to_all | solution.py:21
  14.9 53.3 %all-gather.2.cloned.1.call-done = f32[20480,64]{0,1:T(8,128)} async-done(((f32[1280,64]{0,1:T(8,128)}), f32[20480,64]{0,1:T(8,128)}) %all-gather.2.cloned.1.call-update) | async-done | bytes 5242896 | tf_op jit(solution)/shard_map/all_gather | solution.py:42
  68.1 4.0 %copy.10 = f32[8,8,16,1280]{3,2,1,0:T(8,128)S(1)} copy(f32[8,8,16,1280]{3,1,2,0:T(8,128)} %bitcast.23) | data formatting | bytes 10485760
  72.2 5.1 %copy.7 = f32[2,8,1280,64]{2,0,3,1:T(2,128)} copy(f32[2,8,1280,64]{2,1,0,3:T(8,128)S(1)} %bitcast.21) | data formatting | bytes 10485760 | tf_op jit(solution)/shard_map/reshape | solution.py:43
  77.3 0.0 all-to-all-done
  77.3 5.1 %all-to-all-start.1 = ((f32[2,8,1280,64]{2,0,3,1:T(2,128)}), f32[2,8,1280,64]{2,0,3,1:T(2,128)}, u32[]{:S(2)}, u32[]{:S(2)}) async-start(f32[2,8,1280,64]{2,0,3,1:T(2,128)} %copy.7), calls=%async_computation.1 | async-start | bytes 10485760 | tf_op jit(solution)/shard_map/all_to_all | solution.py:44
  82.3 1.3 fusion.2
  83.6 11.1 %psum.14 = f32[]{:T(128)} all-reduce(f32[]{:T(128)} %fusion.2), channel_id=1, replica_groups=mesh['row_0'=4,'row_1'=4,'col'=8] {'row_0'}, use_global_device_ids=true, to_apply=%region_1.0 | all-reduce | flops 1 | bytes 8 | tf_op jit(solution)/shard_map/psum | solution.py:29
  94.7 9.3 %psum.15 = f32[]{:T(128)} all-reduce(f32[]{:T(128)} %psum.14), channel_id=1, replica_groups=mesh['row_0'=4,'row_1'=4,'col'=8] {'row_1'}, use_global_device_ids=true, to_apply=%region_2.0 | all-reduce | flops 1 | bytes 8 | tf_op jit(solution)/shard_map/psum | solution.py:29
  104.6 37.3 %all-to-all-done.1 = f32[2,8,1280,64]{2,0,3,1:T(2,128)} async-done(((f32[2,8,1280,64]{2,0,3,1:T(2,128)}), f32[2,8,1280,64]{2,0,3,1:T(2,128)}, u32[]{:S(2)}, u32[]{:S(2)}) %all-to-all-start.1) | async-done | bytes 5242912 | tf_op jit(solution)/shard_map/all_to_all | solution.py:44
  141.9 5.5 %copy.8 = f32[2,8,1280,64]{2,3,1,0:T(8,128)} copy(f32[2,8,1280,64]{2,0,3,1:T(2,128)} %all-to-all-done.1) | data formatting | bytes 10485760 | tf_op jit(solution)/shard_map/all_to_all | solution.py:44
  147.3 8.7 %copy.9 = f32[1280,2,512]{2,1,0:T(2,128)} copy(f32[1280,2,512]{0,2,1:T(8,128)} %bitcast.22) | data formatting | bytes 10485760 | tf_op jit(solution)/shard_map/transpose | solution.py:46
  156.1 7.6 %reshape.26 = f32[2560,512]{1,0:T(8,128)} reshape(f32[1280,2,512]{2,1,0:T(2,128)} %copy.9) | data formatting | bytes 10485760 | tf_op jit(solution)/shard_map/reshape | solution.py:46
  163.7 47.1 %fusion.1 = f32[1280,2560]{1,0:T(8,128)} fusion(f32[1280,2560]{1,0:T(8,128)} %param.3, f32[1280,512]{0,1:T(8,128)S(1)} %bitcast.20, f32[2560,512]{1,0:T(8,128)} %reshape.26, s32[2560]{0:T(1024)S(1)} %multiply_add_fusion, f32[]{:T(128)S(6)} %div.3, s32[1280]{0:T(1024)S(1)} %multiply_add_fusion.1), kind=kOutput, calls=%fused_computation.2 | convolution fusion | flops 20145766400 | bytes 34094084 | tf_op jit(solution)/shard_map/dot_general | solution.py:47
  (2 shorter events, 0.0 us)
Async XLA Ops:
  6.5 61.6 %all-gather.2.cloned.1.call-start = ((), (), s32[]{:S(2)}) async-start(), calls=%async_computation.2 | async-start | bytes 5570560 | tf_op jit(solution)/shard_map/all_gather | solution.py:42
  9.9 67.3 %all-to-all-start = ((f32[8,1280,64]{1,2,0:T(8,128)}), f32[8,1280,64]{1,2,0:T(8,128)S(1)}, u32[]{:S(2)}, u32[]{:S(2)}) async-start(f32[8,1280,64]{1,2,0:T(8,128)} %broadcast_in_dim.8), calls=%async_computation | async-start | bytes 5242880 | tf_op jit(solution)/shard_map/all_to_all | solution.py:21
  77.3 64.6 %all-to-all-start.1 = ((f32[2,8,1280,64]{2,0,3,1:T(2,128)}), f32[2,8,1280,64]{2,0,3,1:T(2,128)}, u32[]{:S(2)}, u32[]{:S(2)}) async-start(f32[2,8,1280,64]{2,0,3,1:T(2,128)} %copy.7), calls=%async_computation.1 | async-start | bytes 10485760 | tf_op jit(solution)/shard_map/all_to_all | solution.py:44
Sparse Core Ops, SparseCore 0:
  9.5 58.6 all-gather.1
where the time goes:
time: 220 us; the launch traced here: 218 us
  waiting for transfers between devices  91.2 us (41%)
  matrix products  47.1 us (21%)
  local copies, waits for them, and re-layouts  33.6 us (15%)
  blocking collectives  20.3 us (9%)
  between operations  14.1 us (6%)
  starting transfers between devices  9.99 us (5%)
    all_gather x1, waiting for transfers between devices, on_device(): column_block = lax.all_gather(panel_block, ROW, axis=0, tiled=True)  53.3 us
    dot_general x1, matrix products, on_device(): lax.dot_general(mc_rows, mr_rows, (((1,), (1,)), ((), ())), precision=lax...  47.1 us
    all_to_all x1, waiting for transfers between devices, on_device(): lax.all_to_all(shaped, 'col', split_axis=1, concat_axis=3, tiled=True)  37.3 us
    psum x2, blocking collectives, one_axis_at_a_time(): return functools.reduce(lax.psum, axes, array)  20.3 us
    transpose x1, local copies, waits for them, and re-layouts, on_device(): jnp.transpose(stacked, (1, 0, 2))  8.73 us
    reshape x1, local copies, waits for them, and re-layouts, on_device(): jnp.transpose(stacked, (1, 0, 2))  7.59 us
    all_to_all x1, local copies, waits for them, and re-layouts, on_device(): lax.all_to_all(shaped, 'col', split_axis=1, concat_axis=3, tiled=True)  5.46 us
    all_to_all x1, starting transfers between devices, on_device(): lax.all_to_all(shaped, 'col', split_axis=1, concat_axis=3, tiled=True)  5.07 us
  transfers between devices with their start and end apart: 3, of which 2 were waited for; matrix products, arithmetic and copies ran while one was open for 6% of the time, Pallas kernels for 0%

commit v1 on v0

v1 whole, which is shorter than its diff:
```python
import functools

import jax
import jax.numpy as jnp
from jax import lax
from jax.experimental import pallas as pl
from jax.experimental.pallas import tpu as pltpu
from jax.sharding import PartitionSpec as P

N = 20480
MESH = pl.DeviceIdType.MESH
LAG = 2
CHUNKS = 16
DEEPEST = 5
STEPS = CHUNKS + LAG * DEEPEST
TREE = {
    (0, 0): (0, (0,)),
    (1, 0): (1, (0, 1, 3)),
    (1, 3): (2, (0, 2, 3)),
    (1, 1): (2, (2,)),
    (2, 0): (2, (0, 1)),
    (2, 3): (3, (0,)),
    (1, 2): (3, (2,)),
    (0, 1): (3, ()),
    (0, 3): (3, ()),
    (2, 1): (3, (0, 1)),
    (3, 0): (3, ()),
    (2, 2): (4, (0,)),
    (0, 2): (4, ()),
    (3, 1): (4, ()),
    (3, 3): (4, ()),
    (3, 2): (5, ()),
}


def look_up(index, table):
    found = jnp.int32(0)
    for key, value in enumerate(table):
        found = jnp.where(index == key, jnp.int32(value), found)
    return found


def gather_kernel(
    block_ref, trailing_ref,
    t_ref, ah_ref, al_ref, bh_ref, bl_ref, sum_ref,
    at, b32, weave, sq_mine, sq_got,
    load_sem, trailing_sem, copy_sem, y_send, y_recv, d_send, d_recv,
    tree_send, tree_recv, sq_send, sq_recv,
):
    row = lax.axis_index("row")
    col = lax.axis_index("col")
    x, z = row // 4, row % 4
    y, core = col // 2, col % 2

    def device(dx=0, dy=0, dz=0):
        return ((x + dx) % 4 * 4 + (z + dz) % 4, (y + dy) % 4 * 2 + core)

    partner = (row, y * 2 + 1 - core)
    y_up, y_down = device(dy=1), device(dy=3)
    around = (device(dx=1), device(dz=1), device(dx=3), device(dz=3))

    trailing_copy = pltpu.make_async_copy(trailing_ref, t_ref, trailing_sem)
    own = pl.multiple_of(col * 64, 64)
    load = pltpu.make_async_copy(block_ref, at.at[pl.ds(own, 64)], load_sem)
    load.start()
    barrier = pltpu.get_barrier_semaphore()
    for peer in (partner, y_up, y_down, *around):
        pl.semaphore_signal(barrier, inc=1, device_id=peer, device_id_type=MESH)
    load.wait()
    trailing_copy.start()
    value = at[pl.ds(own, 64), :]
    square = jnp.sum((value * value).reshape(8, 8, 1280), axis=0)
    total = square[:, 0:128]
    for tile in range(1, 10):
        total = total + square[:, 128 * tile : 128 * tile + 128]
    sq_mine[0] = total
    pl.semaphore_wait(barrier, 7)

    def half(y_off, same, h):
        owner = (y + y_off) % 4 * 2 + (core if same else 1 - core)
        return pl.ds(pl.multiple_of(owner * 64 + 32 * h, 32), 32)

    def send(rows, send_sem, recv_sem, to):
        return pltpu.make_async_remote_copy(
            src_ref=at.at[rows], dst_ref=at.at[rows], send_sem=send_sem, recv_sem=recv_sem,
            device_id=to, device_id_type=MESH,
        )

    for h in (0, 1):
        send(half(0, True, h), y_send.at[0], y_recv.at[2 + h], y_up).start()
        send(half(0, True, h), y_send.at[1], y_recv.at[h], y_down).start()
        send(half(0, True, h), d_send, d_recv.at[h], partner).start()

    def got_y(index, y_off, h):
        send(half(y_off, True, h), y_send.at[0], y_recv.at[index], y_up).wait_recv()

    def got_d(index, y_off, h):
        send(half(y_off, False, h), d_send, d_recv.at[index], partner).wait_recv()

    def over(index, y_off, h):
        send(half(y_off, True, h), d_send, d_recv.at[index], partner).start()

    def quarter(rel):
        return pl.ds(pl.multiple_of((y + rel) % 4 * 128, 128), 128)

    roots = []
    plans = []
    for p in range(2):
        u = (x - (y // 2 + 2 * p)) % 4
        v = (z - (y % 2 * 2 + core)) % 4
        roots.append((u == 0) & (v == 0))
        for t in range(4):
            cu, cv = ((u, v), (v, (4 - u) % 4), ((4 - u) % 4, (4 - v) % 4), ((4 - v) % 4, u))[t]
            table = [TREE[i // 4, i % 4] for i in range(16)]
            code = look_up(cu * 4 + cv, [d + 8 * sum(1 << k for k in kids) for d, kids in table])
            plans.append((p, t, code % 8, code // 8))

    def own_copy(p, rel):
        rows = quarter(rel)
        return pltpu.make_async_copy(at.at[rows], b32.at[p, rows], copy_sem.at[p, rel])

    def convert(rel):
        for p in range(2):
            @pl.when(roots[p])
            def _():
                own_copy(p, rel).wait()
        rows = quarter(rel)
        cols = slice(128 * rel, 128 * rel + 128)

        @pl.loop(0, 10)
        def _(n):
            lanes = pl.ds(pl.multiple_of(n * 128, 128), 128)
            a = at[rows, lanes].T
            high = a.astype(jnp.bfloat16)
            ah_ref[lanes, cols] = high
            al_ref[lanes, cols] = (a - high.astype(jnp.float32)).astype(jnp.bfloat16)
            wide = pl.ds(pl.multiple_of(n * 256, 256), 256)
            for p in range(2):
                weave[n % 2, pl.ds(p, 128, stride=2), :] = b32[p, rows, lanes].T
            b = weave[n % 2]
            high = b.astype(jnp.bfloat16)
            bh_ref[wide, cols] = high
            bl_ref[wide, cols] = (b - high.astype(jnp.float32)).astype(jnp.bfloat16)

    def sq_peer(e):
        flip_x = jnp.where(e == 3, x + 1 - 2 * (x % 2), jnp.where(e == 4, 3 - x, x))
        flip_z = jnp.where(e == 5, z + 1 - 2 * (z % 2), jnp.where(e == 6, 3 - z, z))
        flip_y = jnp.where(e == 1, y + 1 - 2 * (y % 2), jnp.where(e == 2, 3 - y, y))
        flip_core = jnp.where(e == 0, 1 - core, core)
        return (flip_x * 4 + flip_z, flip_y * 2 + flip_core)

    def sq_copy(e):
        return pltpu.make_async_remote_copy(
            src_ref=sq_mine.at[e], dst_ref=sq_got.at[e], send_sem=sq_send.at[e], recv_sem=sq_recv.at[e],
            device_id=sq_peer(e), device_id_type=MESH,
        )

    def chunk_rows(c, t):
        group, low = c // 4, c % 2
        middle = (group == 1) | (group == 2)
        h = jnp.where(middle, group - 1, low)
        y_off = jnp.where(middle, 1 + 2 * low, jnp.where(group == 0, 0, 2))
        owner = (y + y_off) % 4 * 2 + (core + c // 2) % 2
        return pl.ds(pl.multiple_of(owner * 64 + 32 * h + 8 * t, 8), 8)

    @pl.loop(0, STEPS)
    def _(s):
        @pl.when(s == 2)
        def _():
            got_d(0, 0, 0)
            got_d(1, 0, 1)

        @pl.when(s == 4)
        def _():
            got_y(2, 3, 0)
            send(half(3, True, 0), y_send.at[2], y_recv.at[4], y_up).start()
            over(4, 3, 0)
            got_y(0, 1, 0)
            over(2, 1, 0)
            for p in range(2):
                @pl.when(roots[p])
                def _():
                    own_copy(p, 0).start()

        @pl.when(s == 6)
        def _():
            got_d(2, 1, 0)
            got_d(4, 3, 0)

        @pl.when(s == 8)
        def _():
            got_y(1, 1, 1)
            send(half(1, True, 1), y_send.at[3], y_recv.at[5], y_down).start()
            over(3, 1, 1)
            got_y(3, 3, 1)
            over(5, 3, 1)

        @pl.when(s == 10)
        def _():
            got_d(3, 1, 1)
            got_d(5, 3, 1)
            for p in range(2):
                @pl.when(roots[p])
                def _():
                    own_copy(p, 1).start()
                    own_copy(p, 3).start()

        @pl.when(s == 12)
        def _():
            got_y(4, 2, 0)
            over(6, 2, 0)
            got_y(5, 2, 1)
            over(7, 2, 1)

        @pl.when(s == 14)
        def _():
            got_d(6, 2, 0)
            got_d(7, 2, 1)
            for p in range(2):
                @pl.when(roots[p])
                def _():
                    own_copy(p, 2).start()

        for p, t, depth, kids in plans:
            c = s - LAG * depth
            live = (c >= 0) & (c < CHUNKS)
            rows = chunk_rows(c, t)

            def forward(src, d, c=c, rows=rows, p=p, t=t):
                return pltpu.make_async_remote_copy(
                    src_ref=src, dst_ref=b32.at[p, rows],
                    send_sem=tree_send.at[p, t, d], recv_sem=tree_recv.at[p, t, c],
                    device_id=around[(d + t) % 4], device_id_type=MESH,
                )

            @pl.when(live & (depth == 0))
            def _():
                forward(at.at[rows], 0).start()

            @pl.when(live & (depth > 0))
            def _():
                forward(b32.at[p, rows], 0).wait_recv()
                for d in range(4):
                    @pl.when(kids // (1 << d) % 2 == 1)
                    def _():
                        forward(b32.at[p, rows], d).start()

        @pl.when((s % 2 == 0) & (s < 14))
        def _():
            sq_copy(s // 2).start()

        @pl.when((s % 2 == 1) & (s < 14))
        def _():
            e = s // 2
            sq_copy(e).wait_recv()
            sq_mine[e + 1] = sq_mine[e] + sq_got[e]

        @pl.when(s == 3 + LAG * DEEPEST)
        def _():
            convert(0)

        @pl.when(s == 11 + LAG * DEEPEST)
        def _():
            convert(1)

        @pl.when(s == 12 + LAG * DEEPEST)
        def _():
            convert(3)

    convert(2)
    sum_ref[...] = sq_mine[7]

    def sent(sem, rows):
        return pltpu.make_async_remote_copy(
            src_ref=at.at[pl.ds(0, rows)], dst_ref=at.at[pl.ds(0, rows)], send_sem=sem, recv_sem=sem,
            device_id=partner, device_id_type=MESH,
        ).wait_send()

    for p, t, depth, kids in plans:
        for d in range(4):
            @pl.when(kids // (1 << d) % 2 == 1)
            def _():
                sent(tree_send.at[p, t, d], CHUNKS * 8)

    sent(y_send.at[0], 64)
    sent(y_send.at[1], 64)
    sent(y_send.at[2], 32)
    sent(y_send.at[3], 32)
    sent(d_send, 256)

    @pl.loop(0, 7)
    def _(e):
        sq_copy(e).wait_send()

    trailing_copy.wait()


def update_kernel(t_ref, ah_ref, al_ref, bh_ref, bl_ref, sum_ref, out_ref, stage, upper_sem, tile_sem):
    row = lax.axis_index("row")
    col = lax.axis_index("col")
    dot = functools.partial(
        lax.dot_general, dimension_numbers=(((1,), (1,)), ((), ())), preferred_element_type=jnp.float32
    )

    def upper(a):
        where = (pl.ds(256 * a, 256), pl.ds(512 * (a + 1), 2560 - 512 * (a + 1)))
        return pltpu.make_async_copy(t_ref.at[where], out_ref.at[where], upper_sem.at[a])

    def tile_copy(a, b):
        where = (pl.ds(256 * a, 256), pl.ds(512 * b, 512))
        return pltpu.make_async_copy(stage.at[where], out_ref.at[where], tile_sem.at[a, b])

    for a in range(4):
        upper(a).start()
    squares = jnp.sum(sum_ref[...])
    factor = 0.8 * jnp.sqrt(jnp.float32(N)) / jnp.sqrt(jnp.full((256, 512), squares, jnp.float32) + 1e-6)

    @pl.loop(0, 5)
    def _(a):
        @pl.loop(0, a + 1)
        def _(b):
            rows = pl.ds(pl.multiple_of(a * 256, 256), 256)
            cols = pl.ds(pl.multiple_of(b * 512, 512), 512)
            ah, bh = ah_ref[rows, :], bh_ref[cols, :]
            update = dot(ah, bh) + dot(ah, bl_ref[cols, :]) + dot(al_ref[rows, :], bh)
            i = lax.broadcasted_iota(jnp.int32, (256, 512), 0)
            j = lax.broadcasted_iota(jnp.int32, (256, 512), 1)
            lower = (a * 256 + i) * 16 + row >= (b * 512 + j) * 8 + col
            stage[rows, cols] = t_ref[rows, cols] - factor * jnp.where(lower, update, 0.0)
            copy = pltpu.make_async_copy(stage.at[rows, cols], out_ref.at[rows, cols], tile_sem.at[a, b])
            copy.start()

    for a in range(4):
        upper(a).wait()
    for a in range(5):
        for b in range(a + 1):
            tile_copy(a, b).wait()


def on_device(panel_block, trailing):
    bf16 = jnp.bfloat16
    f32 = jnp.float32
    dma = pltpu.SemaphoreType.DMA
    anywhere = pl.BlockSpec(memory_space=pl.ANY)
    vmem = pl.BlockSpec(memory_space=pltpu.VMEM)
    gathered = pl.pallas_call(
        gather_kernel,
        out_shape=(
            pltpu.VMEM((1280, 2560), f32),
            pltpu.VMEM((1280, 512), bf16),
            pltpu.VMEM((1280, 512), bf16),
            pltpu.VMEM((2560, 512), bf16),
            pltpu.VMEM((2560, 512), bf16),
            pltpu.VMEM((8, 128), f32),
        ),
        in_specs=[anywhere, anywhere],
        out_specs=[vmem] * 6,
        scratch_shapes=[
            pltpu.VMEM((512, 1280), f32),
            pltpu.VMEM((2, 512, 1280), f32),
            pltpu.VMEM((2, 256, 128), f32),
            pltpu.VMEM((8, 8, 128), f32),
            pltpu.VMEM((7, 8, 128), f32),
            dma(()), dma(()), dma((2, 4)), dma((4,)), dma((6,)), dma(()), dma((8,)),
            dma((2, 4, 4)), dma((2, 4, CHUNKS)), dma((7,)), dma((7,)),
        ],
        compiler_params=pltpu.CompilerParams(
            collective_id=0, has_side_effects=True, vmem_limit_bytes=12 * 1024 * 1024
        ),
        name="gather",
    )(panel_block.T, trailing)
    return pl.pallas_call(
        update_kernel,
        out_shape=jax.ShapeDtypeStruct((1280, 2560), f32),
        in_specs=[vmem] * 6,
        out_specs=anywhere,
        scratch_shapes=[pltpu.VMEM((1280, 2560), f32), dma((4,)), dma((5, 5))],
        compiler_params=pltpu.CompilerParams(vmem_limit_bytes=24 * 1024 * 1024),
        name="update",
    )(*gathered)


def solution(mesh):
    return jax.shard_map(
        on_device,
        mesh=mesh,
        in_specs=(P("row", "col"), P("row", "col")),
        out_specs=P("row", "col"),
        check_vma=False,
    )
```

time: 220 us -> 79.4 us (0.36)
  the two profiles are of different devices: /device:TPU:8 before, /device:TPU:32 now
where the time goes in v1:
time: 79.4 us; the launch traced here: 79.2 us
  Pallas kernels  73.5 us (93%)
  local copies, waits for them, and re-layouts  5.7 us (7%)
    pallas_call x1, Pallas kernels, on_device(): pl.pallas_call(gather_kernel, out_shape=(pltpu.VMEM((1280, 2560), f32), p...  62.8 us
    pallas_call x1, Pallas kernels, on_device(): pl.pallas_call(update_kernel, out_shape=jax.ShapeDtypeStruct((1280, 2560)...  10.7 us
    unnamed x4, local copies, waits for them, and re-layouts  5.7 us

profile of v1, /device:TPU:32, one launch (start us, length us, event | category | flops | bytes accessed | tf_op | source)
XLA Modules:
  0.0 79.2 jit_solution(4531809436218865901)
XLA Ops:
  0.0 0.0 copy-start
  0.0 4.7 %copy-done = f32[1280,2560]{1,0:T(8,128)S(1)} copy-done((f32[1280,2560]{1,0:T(8,128)S(1)}, f32[1280,2560]{1,0:T(8,128)}, u32[]{:S(2)}) %copy-start) | copy-done | bytes 13107224
  4.7 0.0 copy-start.1
  4.7 1.0 %copy-done.1 = f32[1280,64]{0,1:T(8,128)S(1)} copy-done((f32[1280,64]{0,1:T(8,128)S(1)}, f32[1280,64]{0,1:T(8,128)}, u32[]{:S(2)}) %copy-start.1) | copy-done | bytes 327704
  5.7 62.8 %gather.1 = (f32[1280,2560]{1,0:T(8,128)S(1)}, bf16[1280,512]{1,0:T(8,128)(2,1)S(1)}, bf16[1280,512]{1,0:T(8,128)(2,1)S(1)}, bf16[2560,512]{1,0:T(8,128)(2,1)S(1...) custom-call(f32[64,1280]{1,0:T(8,128)S(1)} %bitcast.1, f32[1280,2560]{1,0:T(8,128)S(1)} %copy-done), custom_call_target="tpu_custom_call" | custom-call | tf_op jit(solution)/shard_map/gather/pallas_call | solution.py:346
  68.5 10.7 %update.1 = f32[1280,2560]{1,0:T(8,128)} custom-call(f32[1280,2560]{1,0:T(8,128)S(1)} %get-tuple-element.11.t_ref, bf16[1280,512]{1,0:T(8,128)(2,1)S(1)} %get-tuple-element.12.ah_ref, bf16[1280,512]{1,0:T(8,128)(2,1)S(1)} %get-tuple-element.13.al_ref, bf16[2560,512]{1,0:T(8,128)(2,1)S(1)} %get-tuple-element.14.bh_ref, ...), custom_call_target="tpu_custom_call" | custom-call | tf_op jit(solution)/shard_map/update/pallas_call | solution.py:372
Async XLA Ops:
  0.0 4.7 %copy-start = (f32[1280,2560]{1,0:T(8,128)S(1)}, f32[1280,2560]{1,0:T(8,128)}, u32[]{:S(2)}) copy-start(f32[1280,2560]{1,0:T(8,128)} %trailing_ref.1) | copy-start | bytes 39321604
  4.7 1.0 %copy-start.1 = (f32[1280,64]{0,1:T(8,128)S(1)}, f32[1280,64]{0,1:T(8,128)}, u32[]{:S(2)}) copy-start(f32[1280,64]{0,1:T(8,128)} %param.2) | copy-start | bytes 983044

commit v2 on v1

--- a/solution.py
+++ b/solution.py
@@ -42,8 +42,8 @@
 
 def gather_kernel(
     block_ref, trailing_ref,
-    t_ref, ah_ref, al_ref, bh_ref, bl_ref, sum_ref,
-    at, b32, weave, sq_mine, sq_got,
+    t_ref, acc_ref, a_last, b_last, sum_ref,
+    at, b32, a_cat, b_cat, weave, sq_mine, sq_got,
     load_sem, trailing_sem, copy_sem, y_send, y_recv, d_send, d_recv,
     tree_send, tree_recv, sq_send, sq_recv,
 ):
@@ -119,28 +119,38 @@
         rows = quarter(rel)
         return pltpu.make_async_copy(at.at[rows], b32.at[p, rows], copy_sem.at[p, rel])
 
-    def convert(rel):
-        for p in range(2):
-            @pl.when(roots[p])
-            def _():
-                own_copy(p, rel).wait()
+    def convert(rel, first=0, last=10):
+        if first == 0:
+            for p in range(2):
+                @pl.when(roots[p])
+                def _():
+                    own_copy(p, rel).wait()
         rows = quarter(rel)
-        cols = slice(128 * rel, 128 * rel + 128)
-
-        @pl.loop(0, 10)
+        a_to, b_to, base = (a_last, b_last, 0) if rel == 2 else (a_cat, b_cat, 384 * (0, 1, None, 2)[rel])
+
+        def split(value):
+            high = value.astype(jnp.bfloat16)
+            return high, (value - high.astype(jnp.float32)).astype(jnp.bfloat16)
+
+        @pl.loop(first, last, unroll=2)
         def _(n):
             lanes = pl.ds(pl.multiple_of(n * 128, 128), 128)
-            a = at[rows, lanes].T
-            high = a.astype(jnp.bfloat16)
-            ah_ref[lanes, cols] = high
-            al_ref[lanes, cols] = (a - high.astype(jnp.float32)).astype(jnp.bfloat16)
+            high, low = split(at[rows, lanes].T)
+            for k, part in enumerate((high, high, low)):
+                a_to[lanes, base + 128 * k : base + 128 * k + 128] = part
+            for p in range(2):
+                weave[n % 2, pl.ds(p, 128, stride=2), :] = b32[p, rows, lanes].T
             wide = pl.ds(pl.multiple_of(n * 256, 256), 256)
-            for p in range(2):
-                weave[n % 2, pl.ds(p, 128, stride=2), :] = b32[p, rows, lanes].T
-            b = weave[n % 2]
-            high = b.astype(jnp.bfloat16)
-            bh_ref[wide, cols] = high
-            bl_ref[wide, cols] = (b - high.astype(jnp.float32)).astype(jnp.bfloat16)
+            high, low = split(weave[n % 2])
+            for k, part in enumerate((high, low, high)):
+                b_to[wide, base + 128 * k : base + 128 * k + 128] = part
+
+    def product(b, start, stop):
+        rows, cols = slice(256 * b, 1280), slice(512 * b, 512 * b + 512)
+        return lax.dot_general(
+            a_cat[rows, start:stop], b_cat[cols, start:stop],
+            (((1,), (1,)), ((), ())), preferred_element_type=jnp.float32,
+        )
 
     def sq_peer(e):
         flip_x = jnp.where(e == 3, x + 1 - 2 * (x % 2), jnp.where(e == 4, 3 - x, x))
@@ -255,18 +265,20 @@
             sq_copy(e).wait_recv()
             sq_mine[e + 1] = sq_mine[e] + sq_got[e]
 
-        @pl.when(s == 3 + LAG * DEEPEST)
-        def _():
-            convert(0)
-
-        @pl.when(s == 11 + LAG * DEEPEST)
-        def _():
-            convert(1)
-
-        @pl.when(s == 12 + LAG * DEEPEST)
-        def _():
-            convert(3)
-
+        ready = 3 + LAG * DEEPEST
+        for k in range(5):
+            @pl.when(s == ready + k)
+            def _():
+                convert(0, 2 * k, 2 * k + 2)
+
+            @pl.when(s == ready + 5 + k)
+            def _():
+                acc_ref[256 * k : 1280, 512 * k : 512 * k + 512] = product(k, 0, 384)
+
+    convert(1)
+    convert(3)
+    for k in range(5):
+        acc_ref[256 * k : 1280, 512 * k : 512 * k + 512] += product(k, 384, 1152)
     convert(2)
     sum_ref[...] = sq_mine[7]
 
@@ -295,46 +307,41 @@
     trailing_copy.wait()
 
 
-def update_kernel(t_ref, ah_ref, al_ref, bh_ref, bl_ref, sum_ref, out_ref, stage, upper_sem, tile_sem):
+def update_kernel(t_ref, acc_ref, a_ref, b_ref, sum_ref, out_ref, stage, upper_sem, lower_sem):
     row = lax.axis_index("row")
     col = lax.axis_index("col")
-    dot = functools.partial(
-        lax.dot_general, dimension_numbers=(((1,), (1,)), ((), ())), preferred_element_type=jnp.float32
-    )
 
     def upper(a):
         where = (pl.ds(256 * a, 256), pl.ds(512 * (a + 1), 2560 - 512 * (a + 1)))
         return pltpu.make_async_copy(t_ref.at[where], out_ref.at[where], upper_sem.at[a])
 
-    def tile_copy(a, b):
-        where = (pl.ds(256 * a, 256), pl.ds(512 * b, 512))
-        return pltpu.make_async_copy(stage.at[where], out_ref.at[where], tile_sem.at[a, b])
+    def lower(b):
+        where = (pl.ds(256 * b, 1280 - 256 * b), pl.ds(512 * b, 512))
+        return pltpu.make_async_copy(stage.at[where], out_ref.at[where], lower_sem.at[b])
 
     for a in range(4):
         upper(a).start()
-    squares = jnp.sum(sum_ref[...])
-    factor = 0.8 * jnp.sqrt(jnp.float32(N)) / jnp.sqrt(jnp.full((256, 512), squares, jnp.float32) + 1e-6)
-
-    @pl.loop(0, 5)
-    def _(a):
-        @pl.loop(0, a + 1)
-        def _(b):
-            rows = pl.ds(pl.multiple_of(a * 256, 256), 256)
-            cols = pl.ds(pl.multiple_of(b * 512, 512), 512)
-            ah, bh = ah_ref[rows, :], bh_ref[cols, :]
-            update = dot(ah, bh) + dot(ah, bl_ref[cols, :]) + dot(al_ref[rows, :], bh)
-            i = lax.broadcasted_iota(jnp.int32, (256, 512), 0)
-            j = lax.broadcasted_iota(jnp.int32, (256, 512), 1)
-            lower = (a * 256 + i) * 16 + row >= (b * 512 + j) * 8 + col
-            stage[rows, cols] = t_ref[rows, cols] - factor * jnp.where(lower, update, 0.0)
-            copy = pltpu.make_async_copy(stage.at[rows, cols], out_ref.at[rows, cols], tile_sem.at[a, b])
-            copy.start()
-
+    squares = jnp.full((8, 512), jnp.sum(sum_ref[...]), jnp.float32)
+    factor = (0.8 * jnp.sqrt(jnp.float32(N)) / jnp.sqrt(squares + 1e-6))[0:1, :]
+    i = lax.broadcasted_iota(jnp.int32, (256, 512), 0)
+    j = lax.broadcasted_iota(jnp.int32, (256, 512), 1)
+    for b in range(5):
+        cols = slice(512 * b, 512 * b + 512)
+        update = acc_ref[256 * b : 1280, cols] + lax.dot_general(
+            a_ref[256 * b : 1280, :], b_ref[cols, :],
+            (((1,), (1,)), ((), ())), preferred_element_type=jnp.float32,
+        )
+        edge = slice(256 * b, 256 * b + 256)
+        below = (256 * b + i) * 16 + row >= (512 * b + j) * 8 + col
+        stage[edge, cols] = t_ref[edge, cols] - factor * jnp.where(below, update[0:256], 0.0)
+        if b < 4:
+            rest = slice(256 * b + 256, 1280)
+            stage[rest, cols] = t_ref[rest, cols] - factor * update[256:]
+        lower(b).start()
     for a in range(4):
         upper(a).wait()
-    for a in range(5):
-        for b in range(a + 1):
-            tile_copy(a, b).wait()
+    for b in range(5):
+        lower(b).wait()
 
 
 def on_device(panel_block, trailing):
@@ -342,22 +349,24 @@
     f32 = jnp.float32
     dma = pltpu.SemaphoreType.DMA
     anywhere = pl.BlockSpec(memory_space=pl.ANY)
+    in_hbm = functools.partial(pltpu.with_memory_space_constraint, memory_space=pltpu.HBM)
     vmem = pl.BlockSpec(memory_space=pltpu.VMEM)
     gathered = pl.pallas_call(
         gather_kernel,
         out_shape=(
             pltpu.VMEM((1280, 2560), f32),
-            pltpu.VMEM((1280, 512), bf16),
-            pltpu.VMEM((1280, 512), bf16),
-            pltpu.VMEM((2560, 512), bf16),
-            pltpu.VMEM((2560, 512), bf16),
+            pltpu.VMEM((1280, 2560), f32),
+            pltpu.VMEM((1280, 384), bf16),
+            pltpu.VMEM((2560, 384), bf16),
             pltpu.VMEM((8, 128), f32),
         ),
         in_specs=[anywhere, anywhere],
-        out_specs=[vmem] * 6,
+        out_specs=[vmem] * 5,
         scratch_shapes=[
             pltpu.VMEM((512, 1280), f32),
             pltpu.VMEM((2, 512, 1280), f32),
+            pltpu.VMEM((1280, 1152), bf16),
+            pltpu.VMEM((2560, 1152), bf16),
             pltpu.VMEM((2, 256, 128), f32),
             pltpu.VMEM((8, 8, 128), f32),
             pltpu.VMEM((7, 8, 128), f32),
@@ -365,16 +374,16 @@
             dma((2, 4, 4)), dma((2, 4, CHUNKS)), dma((7,)), dma((7,)),
         ],
         compiler_params=pltpu.CompilerParams(
-            collective_id=0, has_side_effects=True, vmem_limit_bytes=12 * 1024 * 1024
+            collective_id=0, has_side_effects=True, vmem_limit_bytes=24 * 1024 * 1024
         ),
         name="gather",
-    )(panel_block.T, trailing)
+    )(in_hbm(panel_block.T), in_hbm(trailing))
     return pl.pallas_call(
         update_kernel,
         out_shape=jax.ShapeDtypeStruct((1280, 2560), f32),
-        in_specs=[vmem] * 6,
+        in_specs=[vmem] * 5,
         out_specs=anywhere,
-        scratch_shapes=[pltpu.VMEM((1280, 2560), f32), dma((4,)), dma((5, 5))],
+        scratch_shapes=[pltpu.VMEM((1280, 2560), f32), dma((4,)), dma((5,))],
         compiler_params=pltpu.CompilerParams(vmem_limit_bytes=24 * 1024 * 1024),
         name="update",
     )(*gathered)

time: 79.4 us -> 71.1 us (0.90)
  local copies, waits for them, and re-layouts: 5.7 us -> 0 us
  Pallas kernels: 73.5 us -> 70.9 us
    unnamed x4 -> x0, local copies, waits for them, and re-layouts: 5.7 us -> none
    pallas_call x1, Pallas kernels: 10.7 us -> 5.27 us  [on_device(): pl.pallas_call(update_kernel, out_shape=jax.ShapeDtypeStruct((1280, 2560)...]
    pallas_call x1, Pallas kernels: 62.8 us -> 65.7 us  [on_device(): pl.pallas_call(gather_kernel, out_shape=(pltpu.VMEM((1280, 2560), f32), p...]
where the time goes in v2:
time: 71.1 us; the launch traced here: 71 us
  Pallas kernels  70.9 us (100%)
    pallas_call x1, Pallas kernels, on_device(): pl.pallas_call(gather_kernel, out_shape=(pltpu.VMEM((1280, 2560), f32), p...  65.7 us
    pallas_call x1, Pallas kernels, on_device(): pl.pallas_call(update_kernel, out_shape=jax.ShapeDtypeStruct((1280, 2560)...  5.27 us

profile of v2, /device:TPU:32, one launch (start us, length us, event | category | flops | bytes accessed | tf_op | source)
XLA Modules:
  0.0 71.0 jit_solution(10542282448560037926)
XLA Ops:
  0.0 65.7 %gather.1 = (f32[1280,2560]{1,0:T(8,128)S(1)}, f32[1280,2560]{1,0:T(8,128)S(1)}, bf16[1280,384]{1,0:T(8,128)(2,1)S(1)}, bf16[2560,384]{1,0:T(8,128)(2,1)S(1)}, f32[8,128]{1,0:T(8,128)S(1)}) custom-call(f32[64,1280]{1,0:T(8,128)} %bitcast.1, f32[1280,2560]{1,0:T(8,128)} %trailing_ref.1), custom_call_target="tpu_custom_call" | custom-call | tf_op jit(solution)/shard_map/gather/pallas_call | solution.py:354
  65.7 5.3 %update.1 = f32[1280,2560]{1,0:T(8,128)} custom-call(f32[1280,2560]{1,0:T(8,128)S(1)} %get-tuple-element.10.t_ref, f32[1280,2560]{1,0:T(8,128)S(1)} %get-tuple-element.11.acc_ref, bf16[1280,384]{1,0:T(8,128)(2,1)S(1)} %get-tuple-element.12.a_ref, bf16[2560,384]{1,0:T(8,128)(2,1)S(1)} %get-tuple-element.13.b_ref, f32[8,128]{1,0:T(8,128)S(1)} %get-tuple-element.14.sum_ref), custom_call_target="tpu_custom_call" | custom-call | tf_op jit(solution)/shard_map/update/pallas_call | solution.py:381

commit v3 on v2

--- a/solution.py
+++ b/solution.py
@@ -67,6 +67,23 @@
     for peer in (partner, y_up, y_down, *around):
         pl.semaphore_signal(barrier, inc=1, device_id=peer, device_id_type=MESH)
     load.wait()
+    pl.semaphore_wait(barrier, 7)
+
+    def half(y_off, same, h):
+        owner = (y + y_off) % 4 * 2 + (core if same else 1 - core)
+        return pl.ds(pl.multiple_of(owner * 64 + 32 * h, 32), 32)
+
+    def send(rows, send_sem, recv_sem, to):
+        return pltpu.make_async_remote_copy(
+            src_ref=at.at[rows], dst_ref=at.at[rows], send_sem=send_sem, recv_sem=recv_sem,
+            device_id=to, device_id_type=MESH,
+        )
+
+    for h in (0, 1):
+        send(half(0, True, h), y_send.at[0], y_recv.at[2 + h], y_up).start()
+        send(half(0, True, h), y_send.at[1], y_recv.at[h], y_down).start()
+        send(half(0, True, h), d_send, d_recv.at[h], partner).start()
+
     trailing_copy.start()
     value = at[pl.ds(own, 64), :]
     square = jnp.sum((value * value).reshape(8, 8, 1280), axis=0)
@@ -74,22 +91,6 @@
     for tile in range(1, 10):
         total = total + square[:, 128 * tile : 128 * tile + 128]
     sq_mine[0] = total
-    pl.semaphore_wait(barrier, 7)
-
-    def half(y_off, same, h):
-        owner = (y + y_off) % 4 * 2 + (core if same else 1 - core)
-        return pl.ds(pl.multiple_of(owner * 64 + 32 * h, 32), 32)
-
-    def send(rows, send_sem, recv_sem, to):
-        return pltpu.make_async_remote_copy(
-            src_ref=at.at[rows], dst_ref=at.at[rows], send_sem=send_sem, recv_sem=recv_sem,
-            device_id=to, device_id_type=MESH,
-        )
-
-    for h in (0, 1):
-        send(half(0, True, h), y_send.at[0], y_recv.at[2 + h], y_up).start()
-        send(half(0, True, h), y_send.at[1], y_recv.at[h], y_down).start()
-        send(half(0, True, h), d_send, d_recv.at[h], partner).start()
 
     def got_y(index, y_off, h):
         send(half(y_off, True, h), y_send.at[0], y_recv.at[index], y_up).wait_recv()
@@ -255,13 +256,13 @@
                     def _():
                         forward(b32.at[p, rows], d).start()
 
-        @pl.when((s % 2 == 0) & (s < 14))
-        def _():
-            sq_copy(s // 2).start()
-
-        @pl.when((s % 2 == 1) & (s < 14))
-        def _():
-            e = s // 2
+        @pl.when((s % 3 == 0) & (s < 21))
+        def _():
+            sq_copy(s // 3).start()
+
+        @pl.when((s % 3 == 2) & (s < 21))
+        def _():
+            e = s // 3
             sq_copy(e).wait_recv()
             sq_mine[e + 1] = sq_mine[e] + sq_got[e]
 
@@ -271,14 +272,29 @@
             def _():
                 convert(0, 2 * k, 2 * k + 2)
 
-            @pl.when(s == ready + 5 + k)
+            @pl.when(s == ready + 5 + k // 2)
             def _():
                 acc_ref[256 * k : 1280, 512 * k : 512 * k + 512] = product(k, 0, 384)
 
-    convert(1)
-    convert(3)
-    for k in range(5):
-        acc_ref[256 * k : 1280, 512 * k : 512 * k + 512] += product(k, 384, 1152)
+        @pl.when(s == ready + 8)
+        def _():
+            convert(1)
+
+        @pl.when(s == ready + 9)
+        def _():
+            convert(3)
+
+        @pl.when(s == ready + 10)
+        def _():
+            for k in (0, 1):
+                acc_ref[256 * k : 1280, 512 * k : 512 * k + 512] += product(k, 384, 1152)
+
+        @pl.when(s == ready + 11)
+        def _():
+            for k in (2, 3, 4):
+                acc_ref[256 * k : 1280, 512 * k : 512 * k + 512] += product(k, 384, 1152)
+
+
     convert(2)
     sum_ref[...] = sq_mine[7]
 

time: 71.1 us -> 62.9 us (0.88)
  the two profiles are of different devices: /device:TPU:32 before, /device:TPU:8 now
where the time goes in v3:
time: 62.9 us; the launch traced here: 61.7 us
  Pallas kernels  61.7 us (98%)
    pallas_call x1, Pallas kernels, on_device(): pl.pallas_call(gather_kernel, out_shape=(pltpu.VMEM((1280, 2560), f32), p...  56.4 us
    pallas_call x1, Pallas kernels, on_device(): pl.pallas_call(update_kernel, out_shape=jax.ShapeDtypeStruct((1280, 2560)...  5.27 us

profile of v3, /device:TPU:8, one launch (start us, length us, event | category | flops | bytes accessed | tf_op | source)
XLA Modules:
  0.0 61.7 jit_solution(961633433967795142)
XLA Ops:
  0.0 56.4 %gather.1 = (f32[1280,2560]{1,0:T(8,128)S(1)}, f32[1280,2560]{1,0:T(8,128)S(1)}, bf16[1280,384]{1,0:T(8,128)(2,1)S(1)}, bf16[2560,384]{1,0:T(8,128)(2,1)S(1)}, f32[8,128]{1,0:T(8,128)S(1)}) custom-call(f32[64,1280]{1,0:T(8,128)} %bitcast.1, f32[1280,2560]{1,0:T(8,128)} %trailing_ref.1), custom_call_target="tpu_custom_call" | custom-call | tf_op jit(solution)/shard_map/gather/pallas_call | solution.py:370
  56.4 5.3 %update.1 = f32[1280,2560]{1,0:T(8,128)} custom-call(f32[1280,2560]{1,0:T(8,128)S(1)} %get-tuple-element.10.t_ref, f32[1280,2560]{1,0:T(8,128)S(1)} %get-tuple-element.11.acc_ref, bf16[1280,384]{1,0:T(8,128)(2,1)S(1)} %get-tuple-element.12.a_ref, bf16[2560,384]{1,0:T(8,128)(2,1)S(1)} %get-tuple-element.13.b_ref, f32[8,128]{1,0:T(8,128)S(1)} %get-tuple-element.14.sum_ref), custom_call_target="tpu_custom_call" | custom-call | tf_op jit(solution)/shard_map/update/pallas_call | solution.py:397

commit v4 on v3

--- a/solution.py
+++ b/solution.py
@@ -11,8 +11,8 @@
 MESH = pl.DeviceIdType.MESH
 LAG = 2
 CHUNKS = 16
-DEEPEST = 5
-STEPS = CHUNKS + LAG * DEEPEST
+INNER = 4
+STEPS = CHUNKS + LAG * INNER
 TREE = {
     (0, 0): (0, (0,)),
     (1, 0): (1, (0, 1, 3)),
@@ -33,6 +33,13 @@
 }
 
 
+def encode(u, v):
+    depth, kids = TREE[u, v]
+    step = ((1, 0), (0, 1), (3, 0), (0, 3))
+    ends = [k for k in kids if not TREE[(u + step[k][0]) % 4, (v + step[k][1]) % 4][1]]
+    return depth + 8 * sum(1 << k for k in kids) + 128 * sum(1 << k for k in ends)
+
+
 def look_up(index, table):
     found = jnp.int32(0)
     for key, value in enumerate(table):
@@ -112,9 +119,8 @@
         roots.append((u == 0) & (v == 0))
         for t in range(4):
             cu, cv = ((u, v), (v, (4 - u) % 4), ((4 - u) % 4, (4 - v) % 4), ((4 - v) % 4, u))[t]
-            table = [TREE[i // 4, i % 4] for i in range(16)]
-            code = look_up(cu * 4 + cv, [d + 8 * sum(1 << k for k in kids) for d, kids in table])
-            plans.append((p, t, code % 8, code // 8))
+            code = look_up(cu * 4 + cv, [encode(i // 4, i % 4) for i in range(16)])
+            plans.append((p, t, code % 8, code // 8 % 16, code // 128))
 
     def own_copy(p, rel):
         rows = quarter(rel)
@@ -153,6 +159,21 @@
             (((1,), (1,)), ((), ())), preferred_element_type=jnp.float32,
         )
 
+    def multiply(start, stop, *blocks):
+        for k in blocks:
+            where = (slice(256 * k, 1280), slice(512 * k, 512 * k + 512))
+            if start == 0:
+                acc_ref[where] = product(k, start, stop)
+            else:
+                acc_ref[where] += product(k, start, stop)
+
+    def ended(group):
+        rows = pl.ds(0, (32, 64, 32)[group])
+        for p, t, depth, kids, ends in plans:
+            @pl.when(kids == 0)
+            def _():
+                pltpu.make_async_copy(b32.at[p, rows], b32.at[p, rows], tree_recv.at[p, t, 16 + group]).wait()
+
     def sq_peer(e):
         flip_x = jnp.where(e == 3, x + 1 - 2 * (x % 2), jnp.where(e == 4, 3 - x, x))
         flip_z = jnp.where(e == 5, z + 1 - 2 * (z % 2), jnp.where(e == 6, 3 - z, z))
@@ -232,15 +253,16 @@
                 def _():
                     own_copy(p, 2).start()
 
-        for p, t, depth, kids in plans:
+        for p, t, depth, kids, ends in plans:
             c = s - LAG * depth
             live = (c >= 0) & (c < CHUNKS)
             rows = chunk_rows(c, t)
-
-            def forward(src, d, c=c, rows=rows, p=p, t=t):
+            late = 16 + jnp.where(c >= 4, 1, 0) + jnp.where(c >= 12, 1, 0) - c
+
+            def forward(src, d, c=c, rows=rows, p=p, t=t, late=late, ends=ends):
                 return pltpu.make_async_remote_copy(
                     src_ref=src, dst_ref=b32.at[p, rows],
-                    send_sem=tree_send.at[p, t, d], recv_sem=tree_recv.at[p, t, c],
+                    send_sem=tree_send.at[p, t, d], recv_sem=tree_recv.at[p, t, c + late * (ends // (1 << d) % 2)],
                     device_id=around[(d + t) % 4], device_id_type=MESH,
                 )
 
@@ -248,9 +270,9 @@
             def _():
                 forward(at.at[rows], 0).start()
 
-            @pl.when(live & (depth > 0))
-            def _():
-                forward(b32.at[p, rows], 0).wait_recv()
+            @pl.when(live & (depth > 0) & (kids > 0))
+            def _():
+                pltpu.make_async_copy(b32.at[p, rows], b32.at[p, rows], tree_recv.at[p, t, c]).wait()
                 for d in range(4):
                     @pl.when(kids // (1 << d) % 2 == 1)
                     def _():
@@ -266,7 +288,12 @@
             sq_copy(e).wait_recv()
             sq_mine[e + 1] = sq_mine[e] + sq_got[e]
 
-        ready = 3 + LAG * DEEPEST
+        ready = 3 + LAG * (INNER + 1)
+
+        @pl.when(s == ready)
+        def _():
+            ended(0)
+
         for k in range(5):
             @pl.when(s == ready + k)
             def _():
@@ -274,10 +301,11 @@
 
             @pl.when(s == ready + 5 + k // 2)
             def _():
-                acc_ref[256 * k : 1280, 512 * k : 512 * k + 512] = product(k, 0, 384)
+                multiply(0, 384, k)
 
         @pl.when(s == ready + 8)
         def _():
+            ended(1)
             convert(1)
 
         @pl.when(s == ready + 9)
@@ -286,15 +314,10 @@
 
         @pl.when(s == ready + 10)
         def _():
-            for k in (0, 1):
-                acc_ref[256 * k : 1280, 512 * k : 512 * k + 512] += product(k, 384, 1152)
-
-        @pl.when(s == ready + 11)
-        def _():
-            for k in (2, 3, 4):
-                acc_ref[256 * k : 1280, 512 * k : 512 * k + 512] += product(k, 384, 1152)
-
-
+            multiply(384, 1152, 0, 1)
+
+    multiply(384, 1152, 2, 3, 4)
+    ended(2)
     convert(2)
     sum_ref[...] = sq_mine[7]
 
@@ -304,7 +327,7 @@
             device_id=partner, device_id_type=MESH,
         ).wait_send()
 
-    for p, t, depth, kids in plans:
+    for p, t, depth, kids, ends in plans:
         for d in range(4):
             @pl.when(kids // (1 << d) % 2 == 1)
             def _():
@@ -387,7 +410,7 @@
             pltpu.VMEM((8, 8, 128), f32),
             pltpu.VMEM((7, 8, 128), f32),
             dma(()), dma(()), dma((2, 4)), dma((4,)), dma((6,)), dma(()), dma((8,)),
-            dma((2, 4, 4)), dma((2, 4, CHUNKS)), dma((7,)), dma((7,)),
+            dma((2, 4, 4)), dma((2, 4, CHUNKS + 3)), dma((7,)), dma((7,)),
         ],
         compiler_params=pltpu.CompilerParams(
             collective_id=0, has_side_effects=True, vmem_limit_bytes=24 * 1024 * 1024

time: 62.9 us -> 61.1 us (0.971); the launches traced: 61.7 us -> 60.9 us
  Pallas kernels: 61.7 us -> 60.9 us
    pallas_call x1, Pallas kernels: 56.4 us -> 55.6 us  [on_device(): pl.pallas_call(gather_kernel, out_shape=(pltpu.VMEM((1280, 2560), f32), p...]
where the time goes in v4:
time: 61.1 us; the launch traced here: 60.9 us
  Pallas kernels  60.9 us (100%)
    pallas_call x1, Pallas kernels, on_device(): pl.pallas_call(gather_kernel, out_shape=(pltpu.VMEM((1280, 2560), f32), p...  55.6 us
    pallas_call x1, Pallas kernels, on_device(): pl.pallas_call(update_kernel, out_shape=jax.ShapeDtypeStruct((1280, 2560)...  5.27 us

profile of v4, /device:TPU:8, one launch (start us, length us, event | category | flops | bytes accessed | tf_op | source)
XLA Modules:
  0.0 60.9 jit_solution(10064109971209689669)
XLA Ops:
  0.0 55.6 %gather.1 = (f32[1280,2560]{1,0:T(8,128)S(1)}, f32[1280,2560]{1,0:T(8,128)S(1)}, bf16[1280,384]{1,0:T(8,128)(2,1)S(1)}, bf16[2560,384]{1,0:T(8,128)(2,1)S(1)}, f32[8,128]{1,0:T(8,128)S(1)}) custom-call(f32[64,1280]{1,0:T(8,128)} %bitcast.1, f32[1280,2560]{1,0:T(8,128)} %trailing_ref.1), custom_call_target="tpu_custom_call" | custom-call | tf_op jit(solution)/shard_map/gather/pallas_call | solution.py:393
  55.7 5.3 %update.1 = f32[1280,2560]{1,0:T(8,128)} custom-call(f32[1280,2560]{1,0:T(8,128)S(1)} %get-tuple-element.10.t_ref, f32[1280,2560]{1,0:T(8,128)S(1)} %get-tuple-element.11.acc_ref, bf16[1280,384]{1,0:T(8,128)(2,1)S(1)} %get-tuple-element.12.a_ref, bf16[2560,384]{1,0:T(8,128)(2,1)S(1)} %get-tuple-element.13.b_ref, f32[8,128]{1,0:T(8,128)S(1)} %get-tuple-element.14.sum_ref), custom_call_target="tpu_custom_call" | custom-call | tf_op jit(solution)/shard_map/update/pallas_call | solution.py:420

commit v5 on v4

--- a/solution.py
+++ b/solution.py
@@ -37,7 +37,9 @@
     depth, kids = TREE[u, v]
     step = ((1, 0), (0, 1), (3, 0), (0, 3))
     ends = [k for k in kids if not TREE[(u + step[k][0]) % 4, (v + step[k][1]) % 4][1]]
-    return depth + 8 * sum(1 << k for k in kids) + 128 * sum(1 << k for k in ends)
+    if not kids:
+        depth = 63
+    return depth + 64 * sum(1 << k for k in kids) + 1024 * sum(1 << k for k in ends)
 
 
 def look_up(index, table):
@@ -120,7 +122,7 @@
         for t in range(4):
             cu, cv = ((u, v), (v, (4 - u) % 4), ((4 - u) % 4, (4 - v) % 4), ((4 - v) % 4, u))[t]
             code = look_up(cu * 4 + cv, [encode(i // 4, i % 4) for i in range(16)])
-            plans.append((p, t, code % 8, code // 8 % 16, code // 128))
+            plans.append((p, t, code % 64, code // 64 % 16, code // 1024))
 
     def own_copy(p, rel):
         rows = quarter(rel)
@@ -255,28 +257,31 @@
 
         for p, t, depth, kids, ends in plans:
             c = s - LAG * depth
-            live = (c >= 0) & (c < CHUNKS)
-            rows = chunk_rows(c, t)
-            late = 16 + jnp.where(c >= 4, 1, 0) + jnp.where(c >= 12, 1, 0) - c
-
-            def forward(src, d, c=c, rows=rows, p=p, t=t, late=late, ends=ends):
-                return pltpu.make_async_remote_copy(
-                    src_ref=src, dst_ref=b32.at[p, rows],
-                    send_sem=tree_send.at[p, t, d], recv_sem=tree_recv.at[p, t, c + late * (ends // (1 << d) % 2)],
-                    device_id=around[(d + t) % 4], device_id_type=MESH,
-                )
-
-            @pl.when(live & (depth == 0))
+
+            @pl.when((c >= 0) & (c < CHUNKS))
             def _():
-                forward(at.at[rows], 0).start()
-
-            @pl.when(live & (depth > 0) & (kids > 0))
-            def _():
-                pltpu.make_async_copy(b32.at[p, rows], b32.at[p, rows], tree_recv.at[p, t, c]).wait()
-                for d in range(4):
-                    @pl.when(kids // (1 << d) % 2 == 1)
-                    def _():
-                        forward(b32.at[p, rows], d).start()
+                rows = chunk_rows(c, t)
+                late = 16 + jnp.where(c >= 4, 1, 0) + jnp.where(c >= 12, 1, 0) - c
+
+                def forward(src, d):
+                    slot = c + late * (ends // (1 << d) % 2)
+                    return pltpu.make_async_remote_copy(
+                        src_ref=src, dst_ref=b32.at[p, rows],
+                        send_sem=tree_send.at[p, t, d], recv_sem=tree_recv.at[p, t, slot],
+                        device_id=around[(d + t) % 4], device_id_type=MESH,
+                    )
+
+                @pl.when(depth == 0)
+                def _():
+                    forward(at.at[rows], 0).start()
+
+                @pl.when(depth > 0)
+                def _():
+                    pltpu.make_async_copy(b32.at[p, rows], b32.at[p, rows], tree_recv.at[p, t, c]).wait()
+                    for d in range(4):
+                        @pl.when(kids // (1 << d) % 2 == 1)
+                        def _():
+                            forward(b32.at[p, rows], d).start()
 
         @pl.when((s % 3 == 0) & (s < 21))
         def _():

time: 61.1 us -> 61 us (level)
  no operation moved by 1% of the time
where the time goes in v5:
time: 61 us; the launch traced here: 60.9 us
  Pallas kernels  60.9 us (100%)
    pallas_call x1, Pallas kernels, on_device(): pl.pallas_call(gather_kernel, out_shape=(pltpu.VMEM((1280, 2560), f32), p...  55.6 us
    pallas_call x1, Pallas kernels, on_device(): pl.pallas_call(update_kernel, out_shape=jax.ShapeDtypeStruct((1280, 2560)...  5.27 us

profile of v5, /device:TPU:8, one launch (start us, length us, event | category | flops | bytes accessed | tf_op | source)
XLA Modules:
  0.0 60.9 jit_solution(6209529282421630454)
XLA Ops:
  0.0 55.6 %gather.1 = (f32[1280,2560]{1,0:T(8,128)S(1)}, f32[1280,2560]{1,0:T(8,128)S(1)}, bf16[1280,384]{1,0:T(8,128)(2,1)S(1)}, bf16[2560,384]{1,0:T(8,128)(2,1)S(1)}, f32[8,128]{1,0:T(8,128)S(1)}) custom-call(f32[64,1280]{1,0:T(8,128)} %bitcast.1, f32[1280,2560]{1,0:T(8,128)} %trailing_ref.1), custom_call_target="tpu_custom_call" | custom-call | tf_op jit(solution)/shard_map/gather/pallas_call | solution.py:398
  55.6 5.3 %update.1 = f32[1280,2560]{1,0:T(8,128)} custom-call(f32[1280,2560]{1,0:T(8,128)S(1)} %get-tuple-element.10.t_ref, f32[1280,2560]{1,0:T(8,128)S(1)} %get-tuple-element.11.acc_ref, bf16[1280,384]{1,0:T(8,128)(2,1)S(1)} %get-tuple-element.12.a_ref, bf16[2560,384]{1,0:T(8,128)(2,1)S(1)} %get-tuple-element.13.b_ref, f32[8,128]{1,0:T(8,128)S(1)} %get-tuple-element.14.sum_ref), custom_call_target="tpu_custom_call" | custom-call | tf_op jit(solution)/shard_map/update/pallas_call | solution.py:425

commit v6 on v5

--- a/solution.py
+++ b/solution.py
@@ -141,16 +141,16 @@
             high = value.astype(jnp.bfloat16)
             return high, (value - high.astype(jnp.float32)).astype(jnp.bfloat16)
 
-        @pl.loop(first, last, unroll=2)
+        @pl.loop(first, last, unroll=5 if last - first == 10 else 2)
         def _(n):
             lanes = pl.ds(pl.multiple_of(n * 128, 128), 128)
             high, low = split(at[rows, lanes].T)
             for k, part in enumerate((high, high, low)):
                 a_to[lanes, base + 128 * k : base + 128 * k + 128] = part
             for p in range(2):
-                weave[n % 2, pl.ds(p, 128, stride=2), :] = b32[p, rows, lanes].T
+                weave[n % 5, pl.ds(p, 128, stride=2), :] = b32[p, rows, lanes].T
             wide = pl.ds(pl.multiple_of(n * 256, 256), 256)
-            high, low = split(weave[n % 2])
+            high, low = split(weave[n % 5])
             for k, part in enumerate((high, low, high)):
                 b_to[wide, base + 128 * k : base + 128 * k + 128] = part
 
@@ -322,8 +322,6 @@
             multiply(384, 1152, 0, 1)
 
     multiply(384, 1152, 2, 3, 4)
-    ended(2)
-    convert(2)
     sum_ref[...] = sq_mine[7]
 
     def sent(sem, rows):
@@ -349,6 +347,9 @@
         sq_copy(e).wait_send()
 
     trailing_copy.wait()
+
+    ended(2)
+    convert(2)
 
 
 def update_kernel(t_ref, acc_ref, a_ref, b_ref, sum_ref, out_ref, stage, upper_sem, lower_sem):
@@ -411,7 +412,7 @@
             pltpu.VMEM((2, 512, 1280), f32),
             pltpu.VMEM((1280, 1152), bf16),
             pltpu.VMEM((2560, 1152), bf16),
-            pltpu.VMEM((2, 256, 128), f32),
+            pltpu.VMEM((5, 256, 128), f32),
             pltpu.VMEM((8, 8, 128), f32),
             pltpu.VMEM((7, 8, 128), f32),
             dma(()), dma(()), dma((2, 4)), dma((4,)), dma((6,)), dma(()), dma((8,)),

time: 61 us -> 60.8 us (level)
  no operation moved by 1% of the time
where the time goes in v6:
time: 60.8 us; the launch traced here: 60.7 us
  Pallas kernels  60.7 us (100%)
    pallas_call x1, Pallas kernels, on_device(): pl.pallas_call(gather_kernel, out_shape=(pltpu.VMEM((1280, 2560), f32), p...  55.4 us
    pallas_call x1, Pallas kernels, on_device(): pl.pallas_call(update_kernel, out_shape=jax.ShapeDtypeStruct((1280, 2560)...  5.27 us

profile of v6, /device:TPU:8, one launch (start us, length us, event | category | flops | bytes accessed | tf_op | source)
XLA Modules:
  0.0 60.7 jit_solution(5352312888122766505)
XLA Ops:
  0.0 55.4 %gather.1 = (f32[1280,2560]{1,0:T(8,128)S(1)}, f32[1280,2560]{1,0:T(8,128)S(1)}, bf16[1280,384]{1,0:T(8,128)(2,1)S(1)}, bf16[2560,384]{1,0:T(8,128)(2,1)S(1)}, f32[8,128]{1,0:T(8,128)S(1)}) custom-call(f32[64,1280]{1,0:T(8,128)} %bitcast.1, f32[1280,2560]{1,0:T(8,128)} %trailing_ref.1), custom_call_target="tpu_custom_call" | custom-call | tf_op jit(solution)/shard_map/gather/pallas_call | solution.py:399
  55.4 5.3 %update.1 = f32[1280,2560]{1,0:T(8,128)} custom-call(f32[1280,2560]{1,0:T(8,128)S(1)} %get-tuple-element.10.t_ref, f32[1280,2560]{1,0:T(8,128)S(1)} %get-tuple-element.11.acc_ref, bf16[1280,384]{1,0:T(8,128)(2,1)S(1)} %get-tuple-element.12.a_ref, bf16[2560,384]{1,0:T(8,128)(2,1)S(1)} %get-tuple-element.13.b_ref, f32[8,128]{1,0:T(8,128)S(1)} %get-tuple-element.14.sum_ref), custom_call_target="tpu_custom_call" | custom-call | tf_op jit(solution)/shard_map/update/pallas_call | solution.py:426

commit v7 on v6

--- a/solution.py
+++ b/solution.py
@@ -94,12 +94,6 @@
         send(half(0, True, h), d_send, d_recv.at[h], partner).start()
 
     trailing_copy.start()
-    value = at[pl.ds(own, 64), :]
-    square = jnp.sum((value * value).reshape(8, 8, 1280), axis=0)
-    total = square[:, 0:128]
-    for tile in range(1, 10):
-        total = total + square[:, 128 * tile : 128 * tile + 128]
-    sq_mine[0] = total
 
     def got_y(index, y_off, h):
         send(half(y_off, True, h), y_send.at[0], y_recv.at[index], y_up).wait_recv()
@@ -283,13 +277,22 @@
                         def _():
                             forward(b32.at[p, rows], d).start()
 
-        @pl.when((s % 3 == 0) & (s < 21))
+        @pl.when(s == 0)
+        def _():
+            value = at[pl.ds(own, 64), :]
+            square = jnp.sum((value * value).reshape(8, 8, 1280), axis=0)
+            total = square[:, 0:128]
+            for tile in range(1, 10):
+                total = total + square[:, 128 * tile : 128 * tile + 128]
+            sq_mine[0] = total
+
+        @pl.when((s % 3 == 1) & (s < 20))
         def _():
             sq_copy(s // 3).start()
 
-        @pl.when((s % 3 == 2) & (s < 21))
-        def _():
-            e = s // 3
+        @pl.when((s % 3 == 0) & (s > 0) & (s < 22))
+        def _():
+            e = s // 3 - 1
             sq_copy(e).wait_recv()
             sq_mine[e + 1] = sq_mine[e] + sq_got[e]
 

time: 60.8 us -> 61.1 us (level)
  no operation moved by 1% of the time
where the time goes in v7:
time: 61.1 us; the launch traced here: 61 us
  Pallas kernels  61 us (100%)
    pallas_call x1, Pallas kernels, on_device(): pl.pallas_call(gather_kernel, out_shape=(pltpu.VMEM((1280, 2560), f32), p...  55.7 us
    pallas_call x1, Pallas kernels, on_device(): pl.pallas_call(update_kernel, out_shape=jax.ShapeDtypeStruct((1280, 2560)...  5.27 us

profile of v7, /device:TPU:8, one launch (start us, length us, event | category | flops | bytes accessed | tf_op | source)
XLA Modules:
  0.0 61.0 jit_solution(2082128334747999851)
XLA Ops:
  0.0 55.7 %gather.1 = (f32[1280,2560]{1,0:T(8,128)S(1)}, f32[1280,2560]{1,0:T(8,128)S(1)}, bf16[1280,384]{1,0:T(8,128)(2,1)S(1)}, bf16[2560,384]{1,0:T(8,128)(2,1)S(1)}, f32[8,128]{1,0:T(8,128)S(1)}) custom-call(f32[64,1280]{1,0:T(8,128)} %bitcast.1, f32[1280,2560]{1,0:T(8,128)} %trailing_ref.1), custom_call_target="tpu_custom_call" | custom-call | tf_op jit(solution)/shard_map/gather/pallas_call | solution.py:402
  55.7 5.3 %update.1 = f32[1280,2560]{1,0:T(8,128)} custom-call(f32[1280,2560]{1,0:T(8,128)S(1)} %get-tuple-element.10.t_ref, f32[1280,2560]{1,0:T(8,128)S(1)} %get-tuple-element.11.acc_ref, bf16[1280,384]{1,0:T(8,128)(2,1)S(1)} %get-tuple-element.12.a_ref, bf16[2560,384]{1,0:T(8,128)(2,1)S(1)} %get-tuple-element.13.b_ref, f32[8,128]{1,0:T(8,128)S(1)} %get-tuple-element.14.sum_ref), custom_call_target="tpu_custom_call" | custom-call | tf_op jit(solution)/shard_map/update/pallas_call | solution.py:429
